TPU v7x, 32 devices: a whole 2x2x4 slice. The times are simulated.
32 devices in a mesh: cell: 4 (over z), wide: 8 (over y, x, core).
Axes of the slice: x: 2, y: 2, z: 4, core: 2. Of those that a mesh axis runs over, the one named last changes fastest.
Arguments:
- positions: float32 [3, 4, 64, 128], P(None, 'cell', 'wide'), may hold values from 0 to 1
- rhs: float32 [3, 4, 64, 128], P(None, 'cell', 'wide'), may hold values from -6 to 6
- blob_owner: int32 [4, 64, 128, 1], P('cell', 'wide'), may hold values from 0 to 31; in each aligned block of 1024 rows (0 to 1023, 1024 to 2047, ..., all dimensions but the last counted through in order) at most 128 rows name the same one
- blob_row: int32 [4, 64, 128], P('cell', 'wide'), may hold values from 0 to 31
- blob_arm: float32 [3, 4, 64, 128], P(None, 'cell', 'wide'), may hold values from -1 to 1
- body_inverse: float32 [6, 6, 1024], P(None, None, ('cell', 'wide'))
Outputs:
- blob_forces: float32 [3, 4, 64, 128], P(None, 'cell', 'wide')
- body_motion: float32 [6, 1024], P(None, ('cell', 'wide'))
Inputs may be any that keep to these rules, and one draw needn't show every extreme that they name: `blob_owner`: at most 128 of the blobs of one device have bodies of one owner, and that many in some device.
All inputs are finite; a program needn't handle non-finite values.
Results may differ from a plain program's by a relative error of at most 0.0003.
Values sent between devices are 32-bit elements; how exact they have to be, the bound alone decides.
A program may use at most 64 MiB of HBM per device.

v0:
```python
import functools
import math

import jax
import jax.numpy as jnp
from jax import lax
from jax.experimental import pallas as pl
from jax.experimental.pallas import tpu as pltpu
from jax.sharding import PartitionSpec as P

ITERS = 3
EPS2 = 0.04
KAPPA = 0.3
MESH = pl.DeviceIdType.MESH
F32 = jnp.float32
BF16 = jnp.bfloat16
CHUNK = 32


def split(value):
    high = value.astype(BF16).astype(F32)
    return high, value - high


def total_of(value):
    return jnp.sum(jnp.sum(value, axis=0, keepdims=True), axis=1, keepdims=True)


def kernel(
    ncell, nwide,
    pos_ref, rhs_ref, own_ref, row_ref, arm_ref, inv_ref,
    out_ref, motion_ref,
    ext0, wext, vext, movx, onehot, tpos, acc, bmat, sbuf, rbuf, mbuf, abuf,
    s_send, s_recv, a_send, a_recv, h_send, h_recv,
):
    ndev = ncell * nwide
    cell, wide = lax.axis_index("cell"), lax.axis_index("wide")
    me = cell * nwide + wide
    tiles, lanes = pos_ref.shape[1], pos_ref.shape[2]
    body_dev = inv_ref.shape[1] // 6
    rows = 6 * body_dev
    width = sbuf.shape[2]
    next_row = tiles + 2
    ext = 3 * next_row
    base = next_row + 1
    group = onehot.shape[2] // lanes
    factor = KAPPA / math.sqrt(9 * lanes)

    def peer_of(step):
        peer = lax.rem(me + step, ndev)
        return peer, (peer // nwide, lax.rem(peer, nwide))

    barrier = pltpu.get_barrier_semaphore()

    def greet(step, carry):
        pl.semaphore_signal(barrier, inc=1, device_id=peer_of(step)[1], device_id_type=MESH)
        return carry

    lax.fori_loop(1, ndev, greet, 0)

    own = pl.ds(base, tiles)
    for c in range(3):
        ext0[own, c, :] = pos_ref[c]
        ext0[own, 3 + c, :] = rhs_ref[c]
        ext0[own, 6 + c, :] = arm_ref[c]
    ext0[own, 9, :] = own_ref[...].astype(F32)
    ext0[own, 10, :] = row_ref[...].astype(F32)

    regions = [(dx, dy) for dx in (-1, 0, 1) for dy in (-1, 0, 1) if (dx, dy) != (0, 0)]

    def halo_copies(ref, slot):
        copies = []
        for k, (dx, dy) in enumerate(regions):
            first, count = {-1: (tiles - 1, 1), 0: (0, tiles), 1: (0, 1)}[dy]
            place = (1 + dx) * next_row + {-1: 0, 0: 1, 1: tiles + 1}[dy]
            copies.append(pltpu.make_async_remote_copy(
                src_ref=ref.at[pl.ds(base + first, count)],
                dst_ref=ref.at[pl.ds(place, count)],
                send_sem=h_send.at[slot, k],
                recv_sem=h_recv.at[slot, k],
                device_id=(lax.rem(cell - dx + ncell, ncell), lax.rem(wide - dy + nwide, nwide)),
                device_id_type=MESH,
            ))
        return copies

    def to_owner(step):
        peer, ids = peer_of(step)
        return pltpu.make_async_remote_copy(
            src_ref=sbuf.at[peer], dst_ref=rbuf.at[me],
            send_sem=s_send.at[step], recv_sem=s_recv.at[step],
            device_id=ids, device_id_type=MESH)

    def to_holder(step):
        peer, ids = peer_of(step)
        return pltpu.make_async_remote_copy(
            src_ref=mbuf.at[0], dst_ref=abuf.at[me],
            send_sem=a_send.at[step], recv_sem=a_recv.at[step],
            device_id=ids, device_id_type=MESH)

    def start_all(make):
        def body(step, carry):
            make(step).start()
            return carry
        lax.fori_loop(1, ndev, body, 0)

    def wait_all(make):
        def body(step, carry):
            make(step).wait()
            return carry
        lax.fori_loop(1, ndev, body, 0)

    arms = [arm_ref[c] for c in range(3)]
    row_flat = jnp.concatenate([row_ref[t : t + 1, :] for t in range(tiles)], axis=1)
    own_flat = jnp.concatenate([own_ref[t : t + 1, :] for t in range(tiles)], axis=1)
    nblob = tiles * lanes
    row_mask = lax.broadcasted_iota(jnp.int32, (body_dev, nblob), 0) == row_flat
    owner_hot = jnp.where(
        lax.broadcasted_iota(jnp.int32, (ndev, nblob), 0) == own_flat, 1.0, 0.0
    ).astype(BF16)
    lane_of = lax.broadcasted_iota(jnp.int32, (1, width), 1)

    def partial_sums(field, dots):
        sent = list(field) + [
            arms[1] * field[2] - arms[2] * field[1],
            arms[2] * field[0] - arms[0] * field[2],
            arms[0] * field[1] - arms[1] * field[0],
        ]
        result = jnp.zeros((ndev, width), F32)
        halves = [split(value) for value in sent]
        for part in range(2):
            pieces = []
            for c in range(6):
                value = halves[c][part]
                flat = jnp.concatenate([value[t : t + 1, :] for t in range(tiles)], axis=1)
                pieces.append(jnp.where(row_mask, flat, 0.0).astype(BF16))
            pieces.append(jnp.zeros((width - rows, nblob), BF16))
            spread = jnp.concatenate(pieces, axis=0)
            result = result + lax.dot_general(
                owner_hot, spread, (((1,), (1,)), ((), ())), preferred_element_type=F32)
        return result + scalars(dots)

    def scalars(dots):
        line = jnp.zeros((1, width), F32)
        for k, value in enumerate(dots):
            line = line + jnp.where(lane_of == rows + k, value, 0.0)
        return line

    def scatter_sums(values):
        sbuf[:, 0, :] = values
        rbuf[me] = sbuf[me]
        start_all(to_owner)

    def received(count):
        wait_all(to_owner)
        line = jnp.sum(rbuf[...], axis=0)
        return line, [
            jnp.sum(jnp.where(lane_of == rows + k, line, 0.0), axis=1, keepdims=True)
            for k in range(count)
        ]

    def give_motion(motion):
        mbuf[0] = motion
        abuf[me] = motion
        start_all(to_holder)

    first_field = [rhs_ref[c] for c in range(3)]
    squares = total_of(sum(f * f for f in first_field))
    first_sums = partial_sums(first_field, [squares])
    pl.semaphore_wait(barrier, ndev - 1)
    first_halo = halo_copies(ext0, 0)
    scatter_sums(first_sums)
    for copy in first_halo:
        copy.start()

    lane_row = lax.rem(lax.broadcasted_iota(jnp.int32, (body_dev, rows), 1), body_dev)
    diagonal = lane_row == lax.broadcasted_iota(jnp.int32, (body_dev, rows), 0)
    bmat[...] = jnp.zeros_like(bmat)
    for b in range(6):
        bmat[b * body_dev : (b + 1) * body_dev, 0:rows] = jnp.where(diagonal, inv_ref[b : b + 1, :], 0.0)

    def spread_target(t, carry):
        for c in range(3):
            line = pos_ref[c, pl.ds(t, 1), :]
            tpos[t, c] = jnp.broadcast_to(line, (lanes, lanes)).T
        return carry

    lax.fori_loop(0, tiles, spread_target, 0)

    def solve_motion(line):
        return jnp.dot(line, bmat[...], precision=lax.Precision.HIGHEST, preferred_element_type=F32)

    line, (beta2,) = received(1)
    beta = jnp.sqrt(beta2)
    motions = [solve_motion(line) / beta]
    give_motion(motions[0])
    for copy in first_halo:
        copy.wait()
    vext[0, :, 0:3, :] = ext0[:, 3:6, :] / beta[None]

    def make_hot(chunk, carry):
        for g in range(group):
            ids = ext0[chunk * group + g, 9:10, :].astype(jnp.int32)
            hot = jnp.where(lax.broadcasted_iota(jnp.int32, (ndev, lanes), 0) == ids, 1.0, 0.0).astype(BF16)
            onehot[chunk, 0:ndev, g * lanes : (g + 1) * lanes] = hot
            onehot[chunk, ndev : 2 * ndev, g * lanes : (g + 1) * lanes] = hot
        return carry

    lax.fori_loop(0, ext // group, make_hot, 0)

    def precondition(j):
        wait_all(to_holder)
        high, low = split(abuf[:, 0, :])
        table = jnp.concatenate([high, low], axis=0).T[0:rows].astype(BF16)

        def body(chunk, carry):
            found = jnp.dot(table, onehot[chunk], preferred_element_type=F32)
            for g in range(group):
                tile = chunk * group + g
                ids = ext0[tile, 10:11, :].astype(jnp.int32)
                mask = lax.broadcasted_iota(jnp.int32, (body_dev, lanes), 0) == ids
                m = []
                for a in range(6):
                    part = found[a * body_dev : (a + 1) * body_dev, g * lanes : (g + 1) * lanes]
                    m.append(jnp.sum(jnp.where(mask, part, 0.0), axis=0, keepdims=True))
                r = [ext0[tile, 6 + c : 7 + c, :] for c in range(3)]
                extra = [
                    m[0] + m[4] * r[2] - m[5] * r[1],
                    m[1] + m[5] * r[0] - m[3] * r[2],
                    m[2] + m[3] * r[1] - m[4] * r[0],
                ]
                for c in range(3):
                    movx[j, tile, c : c + 1, :] = vext[j, tile, c : c + 1, :] + extra[c]
            return carry

        lax.fori_loop(0, ext // group, body, 0)

    def mobility(j, slot):
        def body(t, carry):
            def part(q, carry):
                here = pl.ds(pl.multiple_of(q * CHUNK, CHUNK), CHUNK)
                target = [tpos[t, c, here, :] for c in range(3)]
                sums = [jnp.zeros((CHUNK, lanes), F32) for c in range(3)]
                for code in range(9):
                    dx, dy = code // 3 - 1, code % 3 - 1
                    tile = (1 + dx) * next_row + 1 + dy + t
                    shift = (float(dx), float(dy), 0.0)
                    sep = [target[c] - (ext0[tile, c : c + 1, :] + shift[c]) for c in range(3)]
                    force = [movx[j, tile, c : c + 1, :] for c in range(3)]
                    soft = sep[0] * sep[0] + sep[1] * sep[1] + (sep[2] * sep[2] + EPS2)
                    root = lax.rsqrt(soft)
                    cube = root * root * root
                    near = root + EPS2 * cube
                    along = cube * (sep[0] * force[0] + sep[1] * force[1] + sep[2] * force[2])
                    sums = [sums[c] + (near * force[c] + along * sep[c]) for c in range(3)]
                for c in range(3):
                    acc[c, here, :] = sums[c]
                return carry

            lax.fori_loop(0, lanes // CHUNK, part, 0)
            for c in range(3):
                line = jnp.sum(acc[c].T, axis=0, keepdims=True)
                wext[slot, base + t, c : c + 1, :] = movx[j, base + t, c : c + 1, :] + factor * line
            return carry

        lax.fori_loop(0, tiles, body, 0)

    hessen = []
    for j in range(ITERS):
        precondition(j)
        mobility(j, j)
        fresh = [wext[j, own, c, :] for c in range(3)]
        dots = []
        for i in range(j + 1):
            dots.append(total_of(sum(vext[i, own, c, :] * fresh[c] for c in range(3))))
        dots.append(total_of(sum(f * f for f in fresh)))
        last = j == ITERS - 1
        if not last:
            halo = halo_copies(wext.at[j], 1 + j)
            for copy in halo:
                copy.start()
            scatter_sums(partial_sums(fresh, dots))
        else:
            scatter_sums(jnp.broadcast_to(scalars(dots), (ndev, width)))
        line, values = received(j + 2)
        inners, whole = values[:-1], values[-1]
        squared = whole - sum(h * h for h in inners)
        length = jnp.sqrt(squared)
        hessen.append(inners + [length])
        if not last:
            motion = solve_motion(line)
            for i in range(j + 1):
                motion = motion - inners[i] * motions[i]
            motions.append(motion / length)
            give_motion(motions[-1])
            for copy in halo:
                copy.wait()
            value = wext[j]
            for i in range(j + 1):
                value = value - inners[i][None] * vext[i]
            vext[j + 1] = value / length[None]

    def entry(i, j):
        return hessen[j][i] if i <= j + 1 else None

    def normal(a, b):
        return sum(entry(i, a) * entry(i, b) for i in range(min(a, b) + 2))

    lower = [[None] * ITERS for _ in range(ITERS)]
    for a in range(ITERS):
        for b in range(a + 1):
            value = normal(a, b)
            for k in range(b):
                value = value - lower[a][k] * lower[b][k]
            lower[a][b] = jnp.sqrt(value) if a == b else value / lower[b][b]
    mid = []
    for a in range(ITERS):
        value = beta * entry(0, a)
        for k in range(a):
            value = value - lower[a][k] * mid[k]
        mid.append(value / lower[a][a])
    coeffs = [None] * ITERS
    for a in reversed(range(ITERS)):
        value = mid[a]
        for k in range(a + 1, ITERS):
            value = value - lower[k][a] * coeffs[k]
        coeffs[a] = value / lower[a][a]
    for c in range(3):
        out_ref[c] = sum(coeffs[j] * movx[j, own, c, :] for j in range(ITERS))
    motion_ref[...] = sum(coeffs[j] * motions[j] for j in range(ITERS))


def local(positions, rhs, blob_owner, blob_row, blob_arm, body_inverse):
    tiles, lanes = positions.shape[2], positions.shape[3]
    body_dev = body_inverse.shape[2]
    ncell, nwide = lax.axis_size("cell"), lax.axis_size("wide")
    ndev = ncell * nwide
    ext = 3 * (tiles + 2)
    group = 2 if ext % 2 == 0 else 1
    rows = 6 * body_dev
    width = -(-(rows + ITERS + 2) // 128) * 128
    inverse = jnp.transpose(body_inverse, (1, 0, 2)).reshape(6, rows)
    vmem = pl.BlockSpec(memory_space=pltpu.VMEM)
    forces, motion = pl.pallas_call(
        functools.partial(kernel, ncell, nwide),
        out_shape=(
            jax.ShapeDtypeStruct((3, tiles, lanes), F32),
            jax.ShapeDtypeStruct((1, width), F32),
        ),
        in_specs=[vmem] * 6,
        out_specs=(vmem, vmem),
        scratch_shapes=[
            pltpu.VMEM((ext, 16, lanes), F32),
            pltpu.VMEM((ITERS, ext, 4, lanes), F32),
            pltpu.VMEM((ITERS, ext, 4, lanes), F32),
            pltpu.VMEM((ITERS, ext, 4, lanes), F32),
            pltpu.VMEM((ext // group, 2 * ndev, group * lanes), BF16),
            pltpu.VMEM((tiles, 3, lanes, lanes), F32),
            pltpu.VMEM((3, lanes, lanes), F32),
            pltpu.VMEM((width, width), F32),
            pltpu.VMEM((ndev, 1, width), F32),
            pltpu.VMEM((ndev, 1, width), F32),
            pltpu.VMEM((1, 1, width), F32),
            pltpu.VMEM((ndev, 1, width), F32),
            pltpu.SemaphoreType.DMA((ndev,)),
            pltpu.SemaphoreType.DMA((ndev,)),
            pltpu.SemaphoreType.DMA((ndev,)),
            pltpu.SemaphoreType.DMA((ndev,)),
            pltpu.SemaphoreType.DMA((ITERS, 8)),
            pltpu.SemaphoreType.DMA((ITERS, 8)),
        ],
        compiler_params=pltpu.CompilerParams(
            collective_id=0, has_side_effects=True, vmem_limit_bytes=48 * 1024 * 1024
        ),
    )(
        positions[:, 0], rhs[:, 0], blob_owner.reshape(tiles, lanes),
        blob_row.reshape(tiles, lanes), blob_arm[:, 0], inverse,
    )
    return forces[:, None], motion[0, :rows].reshape(6, body_dev)


def solution(mesh):
    in_specs = (
        P(None, "cell", "wide", None),
        P(None, "cell", "wide", None),
        P("cell", "wide", None, None),
        P("cell", "wide", None),
        P(None, "cell", "wide", None),
        P(None, None, ("cell", "wide")),
    )
    out_specs = (P(None, "cell", "wide", None), P(None, ("cell", "wide")))
    return jax.shard_map(local, mesh=mesh, in_specs=in_specs, out_specs=out_specs, check_vma=False)
```

profile of v0, /device:TPU:0, one launch (start us, length us, event | category | flops | bytes accessed | tf_op | source)
XLA Modules:
  0.0 74.7 jit_solution(12329302535885165067)
XLA Ops:
  0.6 0.0 copy-start.2
  0.6 0.7 %copy.8 = f32[6,6,32]{2,1,0:T(8,128)S(1)} copy(f32[6,6,32]{2,0,1:T(8,128)} %bitcast.15) | data formatting | bytes 9216 | tf_op jit(solution)/shard_map/transpose | solution.py:341
  1.4 0.0 copy-start
  1.4 0.0 copy-start.1
  1.4 0.0 copy-start.3
  1.4 0.0 copy-start.4
  1.4 0.1 reshape.15.inv_ref
  1.5 0.0 copy-done.2
  1.5 0.6 copy-done
  2.1 0.0 copy-done.1
  2.1 0.0 copy-done.3
  2.1 0.0 copy-done.4
  2.1 71.2 %shard_map.77 = (f32[3,8,128]{2,1,0:T(8,128)S(1)}, f32[1,256]{1,0:T(1,128)S(1)}) custom-call(f32[3,8,128]{2,1,0:T(8,128)S(1)} %bitcast.10, f32[3,8,128]{2,1,0:T(8,128)S(1)} %bitcast.11, s32[8,128]{1,0:T(8,128)S(1)} %bitcast.13, s32[8,128]{1,0:T(8,128)S(1)} %bitcast.14, f32[3,8,128]{2,1,0:T(8,128)S(1)} %bitcast.12, f32[6,192]{1,0:T(8,128)S(1)} %reshape.15.inv_ref), custom_call_target="tpu_custom_call" | custom-call | tf_op jit(solution)/shard_map/pallas_call | solution.py:343
  73.4 0.7 reshape_squeeze.3
  74.1 0.6 copy.11
  (1 shorter events, 0.0 us)
Async XLA Ops:
  0.6 0.9 %copy-start.2 = (f32[3,1,8,128]{3,2,1,0:T(8,128)S(1)}, f32[3,1,8,128]{3,2,1,0:T(8,128)}, u32[]{:S(2)}) copy-start(f32[3,1,8,128]{3,2,1,0:T(8,128)} %param.10) | copy-start | bytes 36868
  1.4 0.7 copy-start
  1.4 0.7 copy-start.1
  1.4 0.7 copy-start.3
  1.4 0.7 copy-start.4
where the time goes:
time: 74.9 us; the launch traced here: 74.7 us
  Pallas kernels  71.2 us (95%)
  local copies, waits for them, and re-layouts  2.76 us (4%)
    pallas_call x1, Pallas kernels, local(): pl.pallas_call(functools.partial(kernel, ncell, nwide), out_shape=(jax.Sh...  71.2 us

commit v1 on v0

--- a/solution.py
+++ b/solution.py
@@ -30,14 +30,14 @@
     ncell, nwide,
     pos_ref, rhs_ref, own_ref, row_ref, arm_ref, inv_ref,
     out_ref, motion_ref,
-    ext0, wext, vext, movx, onehot, tpos, acc, bmat, sbuf, rbuf, mbuf, abuf,
+    ext0, wext, vext, movx, onehot, tpos, acc, coef, bhigh, blow, sbuf, rbuf, mbuf, abuf,
     s_send, s_recv, a_send, a_recv, h_send, h_recv,
 ):
     ndev = ncell * nwide
     cell, wide = lax.axis_index("cell"), lax.axis_index("wide")
     me = cell * nwide + wide
     tiles, lanes = pos_ref.shape[1], pos_ref.shape[2]
-    body_dev = inv_ref.shape[1] // 6
+    body_dev = inv_ref.shape[2]
     rows = 6 * body_dev
     width = sbuf.shape[2]
     next_row = tiles + 2
@@ -46,17 +46,14 @@
     group = onehot.shape[2] // lanes
     factor = KAPPA / math.sqrt(9 * lanes)
 
-    def peer_of(step):
-        peer = lax.rem(me + step, ndev)
-        return peer, (peer // nwide, lax.rem(peer, nwide))
+    cells = [cell] + [jnp.where(cell + a >= ncell, cell + a - ncell, cell + a) for a in range(1, ncell)]
+    wides = [wide] + [jnp.where(wide + b >= nwide, wide + b - nwide, wide + b) for b in range(1, nwide)]
+    far = sorted(range(ncell), key=lambda a: -min(a, ncell - a))
+    peers = [(cells[a], wides[b]) for a in far for b in range(nwide) if (a, b) != (0, 0)]
 
     barrier = pltpu.get_barrier_semaphore()
-
-    def greet(step, carry):
-        pl.semaphore_signal(barrier, inc=1, device_id=peer_of(step)[1], device_id_type=MESH)
-        return carry
-
-    lax.fori_loop(1, ndev, greet, 0)
+    for ids in peers:
+        pl.semaphore_signal(barrier, inc=1, device_id=ids, device_id_type=MESH)
 
     own = pl.ds(base, tiles)
     for c in range(3):
@@ -83,31 +80,29 @@
             ))
         return copies
 
-    def to_owner(step):
-        peer, ids = peer_of(step)
-        return pltpu.make_async_remote_copy(
-            src_ref=sbuf.at[peer], dst_ref=rbuf.at[me],
-            send_sem=s_send.at[step], recv_sem=s_recv.at[step],
-            device_id=ids, device_id_type=MESH)
-
-    def to_holder(step):
-        peer, ids = peer_of(step)
-        return pltpu.make_async_remote_copy(
-            src_ref=mbuf.at[0], dst_ref=abuf.at[me],
-            send_sem=a_send.at[step], recv_sem=a_recv.at[step],
-            device_id=ids, device_id_type=MESH)
-
-    def start_all(make):
-        def body(step, carry):
-            make(step).start()
-            return carry
-        lax.fori_loop(1, ndev, body, 0)
-
-    def wait_all(make):
-        def body(step, carry):
-            make(step).wait()
-            return carry
-        lax.fori_loop(1, ndev, body, 0)
+    def start_sums():
+        for ids in peers:
+            pltpu.make_async_remote_copy(
+                src_ref=sbuf.at[ids[0] * nwide + ids[1]], dst_ref=rbuf.at[me],
+                send_sem=s_send, recv_sem=s_recv,
+                device_id=ids, device_id_type=MESH).start()
+
+    def wait_sums():
+        whole = pl.ds(0, ndev - 1)
+        pltpu.make_async_copy(rbuf.at[whole], rbuf.at[whole], s_recv).wait()
+        pltpu.make_async_copy(sbuf.at[whole], sbuf.at[whole], s_send).wait()
+
+    def start_motions():
+        for ids in peers:
+            pltpu.make_async_remote_copy(
+                src_ref=mbuf.at[0], dst_ref=abuf.at[me],
+                send_sem=a_send, recv_sem=a_recv,
+                device_id=ids, device_id_type=MESH).start()
+
+    def wait_motions():
+        whole = pl.ds(0, ndev - 1)
+        pltpu.make_async_copy(abuf.at[whole], abuf.at[whole], a_recv).wait()
+        pltpu.make_async_copy(abuf.at[whole], abuf.at[whole], a_send).wait()
 
     arms = [arm_ref[c] for c in range(3)]
     row_flat = jnp.concatenate([row_ref[t : t + 1, :] for t in range(tiles)], axis=1)
@@ -148,10 +143,10 @@
     def scatter_sums(values):
         sbuf[:, 0, :] = values
         rbuf[me] = sbuf[me]
-        start_all(to_owner)
+        start_sums()
 
     def received(count):
-        wait_all(to_owner)
+        wait_sums()
         line = jnp.sum(rbuf[...], axis=0)
         return line, [
             jnp.sum(jnp.where(lane_of == rows + k, line, 0.0), axis=1, keepdims=True)
@@ -161,7 +156,7 @@
     def give_motion(motion):
         mbuf[0] = motion
         abuf[me] = motion
-        start_all(to_holder)
+        start_motions()
 
     first_field = [rhs_ref[c] for c in range(3)]
     squares = total_of(sum(f * f for f in first_field))
@@ -172,11 +167,16 @@
     for copy in first_halo:
         copy.start()
 
-    lane_row = lax.rem(lax.broadcasted_iota(jnp.int32, (body_dev, rows), 1), body_dev)
-    diagonal = lane_row == lax.broadcasted_iota(jnp.int32, (body_dev, rows), 0)
-    bmat[...] = jnp.zeros_like(bmat)
+    bhigh[...] = jnp.zeros_like(bhigh)
+    blow[...] = jnp.zeros_like(blow)
+    square = (body_dev, body_dev)
+    diagonal = lax.broadcasted_iota(jnp.int32, square, 0) == lax.broadcasted_iota(jnp.int32, square, 1)
     for b in range(6):
-        bmat[b * body_dev : (b + 1) * body_dev, 0:rows] = jnp.where(diagonal, inv_ref[b : b + 1, :], 0.0)
+        for a in range(6):
+            high, low = split(inv_ref[a, b : b + 1, :])
+            here = (slice(b * body_dev, (b + 1) * body_dev), slice(a * body_dev, (a + 1) * body_dev))
+            bhigh[here] = jnp.where(diagonal, high, 0.0)
+            blow[here] = jnp.where(diagonal, low, 0.0)
 
     def spread_target(t, carry):
         for c in range(3):
@@ -186,15 +186,40 @@
 
     lax.fori_loop(0, tiles, spread_target, 0)
 
+    def coefficients(t, carry):
+        def part(q, carry):
+            here = pl.ds(pl.multiple_of(q * CHUNK, CHUNK), CHUNK)
+            target = [tpos[t, c, here, :] for c in range(3)]
+            for code in range(9):
+                dx, dy = code // 3 - 1, code % 3 - 1
+                tile = (1 + dx) * next_row + 1 + dy + t
+                shift = (float(dx), float(dy), 0.0)
+                sep = [target[c] - (ext0[tile, c : c + 1, :] + shift[c]) for c in range(3)]
+                soft = sep[0] * sep[0] + sep[1] * sep[1] + (sep[2] * sep[2] + EPS2)
+                root = lax.rsqrt(soft)
+                twice = root * root
+                coef[t * 9 + code, 3, here, :] = root + EPS2 * (twice * root)
+                scale = twice * lax.rsqrt(root)
+                for c in range(3):
+                    coef[t * 9 + code, c, here, :] = scale * sep[c]
+            return carry
+
+        return lax.fori_loop(0, lanes // CHUNK, part, carry)
+
     def solve_motion(line):
-        return jnp.dot(line, bmat[...], precision=lax.Precision.HIGHEST, preferred_element_type=F32)
-
+        high, low = split(line)
+        both = jnp.concatenate([high, low], axis=0).astype(BF16)
+        one = jnp.dot(both, bhigh[...].astype(BF16), preferred_element_type=F32)
+        two = jnp.dot(both, blow[...].astype(BF16), preferred_element_type=F32)
+        return one[0:1] + one[1:2] + two[0:1]
+
+    for copy in first_halo:
+        copy.wait()
+    lax.fori_loop(0, tiles // 2, coefficients, 0)
     line, (beta2,) = received(1)
     beta = jnp.sqrt(beta2)
     motions = [solve_motion(line) / beta]
     give_motion(motions[0])
-    for copy in first_halo:
-        copy.wait()
     vext[0, :, 0:3, :] = ext0[:, 3:6, :] / beta[None]
 
     def make_hot(chunk, carry):
@@ -206,9 +231,10 @@
         return carry
 
     lax.fori_loop(0, ext // group, make_hot, 0)
+    lax.fori_loop(tiles // 2, tiles, coefficients, 0)
 
     def precondition(j):
-        wait_all(to_holder)
+        wait_motions()
         high, low = split(abuf[:, 0, :])
         table = jnp.concatenate([high, low], axis=0).T[0:rows].astype(BF16)
 
@@ -238,20 +264,14 @@
         def body(t, carry):
             def part(q, carry):
                 here = pl.ds(pl.multiple_of(q * CHUNK, CHUNK), CHUNK)
-                target = [tpos[t, c, here, :] for c in range(3)]
                 sums = [jnp.zeros((CHUNK, lanes), F32) for c in range(3)]
                 for code in range(9):
-                    dx, dy = code // 3 - 1, code % 3 - 1
-                    tile = (1 + dx) * next_row + 1 + dy + t
-                    shift = (float(dx), float(dy), 0.0)
-                    sep = [target[c] - (ext0[tile, c : c + 1, :] + shift[c]) for c in range(3)]
+                    tile = (code // 3) * next_row + code % 3 + t
+                    near = coef[t * 9 + code, 3, here, :]
+                    unit = [coef[t * 9 + code, c, here, :] for c in range(3)]
                     force = [movx[j, tile, c : c + 1, :] for c in range(3)]
-                    soft = sep[0] * sep[0] + sep[1] * sep[1] + (sep[2] * sep[2] + EPS2)
-                    root = lax.rsqrt(soft)
-                    cube = root * root * root
-                    near = root + EPS2 * cube
-                    along = cube * (sep[0] * force[0] + sep[1] * force[1] + sep[2] * force[2])
-                    sums = [sums[c] + (near * force[c] + along * sep[c]) for c in range(3)]
+                    along = unit[0] * force[0] + unit[1] * force[1] + unit[2] * force[2]
+                    sums = [sums[c] + (near * force[c] + along * unit[c]) for c in range(3)]
                 for c in range(3):
                     acc[c, here, :] = sums[c]
                 return carry
@@ -326,7 +346,9 @@
         coeffs[a] = value / lower[a][a]
     for c in range(3):
         out_ref[c] = sum(coeffs[j] * movx[j, own, c, :] for j in range(ITERS))
-    motion_ref[...] = sum(coeffs[j] * motions[j] for j in range(ITERS))
+    motion = sum(coeffs[j] * motions[j] for j in range(ITERS))
+    for a in range(6):
+        motion_ref[a : a + 1, :] = motion[:, a * body_dev : (a + 1) * body_dev]
 
 
 def local(positions, rhs, blob_owner, blob_row, blob_arm, body_inverse):
@@ -335,16 +357,15 @@
     ncell, nwide = lax.axis_size("cell"), lax.axis_size("wide")
     ndev = ncell * nwide
     ext = 3 * (tiles + 2)
-    group = 2 if ext % 2 == 0 else 1
+    group = 6 if ext % 6 == 0 else 3
     rows = 6 * body_dev
     width = -(-(rows + ITERS + 2) // 128) * 128
-    inverse = jnp.transpose(body_inverse, (1, 0, 2)).reshape(6, rows)
     vmem = pl.BlockSpec(memory_space=pltpu.VMEM)
     forces, motion = pl.pallas_call(
         functools.partial(kernel, ncell, nwide),
         out_shape=(
             jax.ShapeDtypeStruct((3, tiles, lanes), F32),
-            jax.ShapeDtypeStruct((1, width), F32),
+            jax.ShapeDtypeStruct((6, body_dev), F32),
         ),
         in_specs=[vmem] * 6,
         out_specs=(vmem, vmem),
@@ -356,15 +377,17 @@
             pltpu.VMEM((ext // group, 2 * ndev, group * lanes), BF16),
             pltpu.VMEM((tiles, 3, lanes, lanes), F32),
             pltpu.VMEM((3, lanes, lanes), F32),
+            pltpu.VMEM((9 * tiles, 4, lanes, lanes), F32),
+            pltpu.VMEM((width, width), F32),
             pltpu.VMEM((width, width), F32),
             pltpu.VMEM((ndev, 1, width), F32),
             pltpu.VMEM((ndev, 1, width), F32),
             pltpu.VMEM((1, 1, width), F32),
             pltpu.VMEM((ndev, 1, width), F32),
-            pltpu.SemaphoreType.DMA((ndev,)),
-            pltpu.SemaphoreType.DMA((ndev,)),
-            pltpu.SemaphoreType.DMA((ndev,)),
-            pltpu.SemaphoreType.DMA((ndev,)),
+            pltpu.SemaphoreType.DMA,
+            pltpu.SemaphoreType.DMA,
+            pltpu.SemaphoreType.DMA,
+            pltpu.SemaphoreType.DMA,
             pltpu.SemaphoreType.DMA((ITERS, 8)),
             pltpu.SemaphoreType.DMA((ITERS, 8)),
         ],
@@ -373,9 +396,9 @@
         ),
     )(
         positions[:, 0], rhs[:, 0], blob_owner.reshape(tiles, lanes),
-        blob_row.reshape(tiles, lanes), blob_arm[:, 0], inverse,
+        blob_row.reshape(tiles, lanes), blob_arm[:, 0], body_inverse,
     )
-    return forces[:, None], motion[0, :rows].reshape(6, body_dev)
+    return forces[:, None], motion
 
 
 def solution(mesh):

time: 74.9 us -> 69.4 us (0.927)
  Pallas kernels: 71.2 us -> 63.5 us
  local copies, waits for them, and re-layouts: 2.76 us -> 4.74 us
    pallas_call x1, Pallas kernels: 71.2 us -> 63.5 us  [local(): pl.pallas_call(functools.partial(kernel, ncell, nwide), out_shape=(jax.Sh...]
    unnamed x11 -> x14, local copies, waits for them, and re-layouts: 1.24 us -> 4.74 us
    transpose x1 -> x0, local copies, waits for them, and re-layouts: 0.75 us -> none  [local(): inverse = jnp.transpose(body_inverse, (1, 0, 2)).reshape(6, rows)]
where the time goes in v1:
time: 69.4 us; the launch traced here: 68.9 us
  Pallas kernels  63.5 us (91%)
  local copies, waits for them, and re-layouts  4.74 us (7%)
    pallas_call x1, Pallas kernels, local(): pl.pallas_call(functools.partial(kernel, ncell, nwide), out_shape=(jax.Sh...  63.5 us
    unnamed x14, local copies, waits for them, and re-layouts  4.74 us

profile of v1, /device:TPU:0, one launch (start us, length us, event | category | flops | bytes accessed | tf_op | source)
XLA Modules:
  0.0 68.9 jit_solution(18295844586526436709)
XLA Ops:
  0.6 0.0 copy-start.5
  0.6 0.0 copy-start.4
  0.7 0.7 copy-done.5
  1.3 0.0 copy-done.4
  1.3 0.0 copy-start
  1.3 0.7 %copy-done = f32[6,6,32]{2,1,0:T(8,128)S(1)} copy-done((f32[6,6,32]{2,1,0:T(8,128)S(1)}, f32[6,6,32]{2,1,0:T(8,128)}, u32[]{:S(2)}) %copy-start) | copy-done | bytes 4632
  2.1 0.0 copy-start.1
  2.1 0.7 %copy-done.1 = f32[3,1,8,128]{3,2,1,0:T(8,128)S(1)} copy-done((f32[3,1,8,128]{3,2,1,0:T(8,128)S(1)}, f32[3,1,8,128]{3,2,1,0:T(8,128)}, u32[]{:S(2)}) %copy-start.1) | copy-done | bytes 12312
  2.8 0.0 copy-start.2
  2.8 0.7 %copy-done.2 = f32[3,1,8,128]{3,2,1,0:T(8,128)S(1)} copy-done((f32[3,1,8,128]{3,2,1,0:T(8,128)S(1)}, f32[3,1,8,128]{3,2,1,0:T(8,128)}, u32[]{:S(2)}) %copy-start.2) | copy-done | bytes 12312
  3.5 0.0 copy-start.3
  3.5 0.7 %copy-done.3 = f32[3,1,8,128]{3,2,1,0:T(8,128)S(1)} copy-done((f32[3,1,8,128]{3,2,1,0:T(8,128)S(1)}, f32[3,1,8,128]{3,2,1,0:T(8,128)}, u32[]{:S(2)}) %copy-start.3) | copy-done | bytes 12312
  4.2 63.5 %shard_map.77 = (f32[3,8,128]{2,1,0:T(8,128)S(1)}, f32[6,32]{1,0:T(8,128)S(1)}) custom-call(f32[3,8,128]{2,1,0:T(8,128)S(1)} %bitcast.9, f32[3,8,128]{2,1,0:T(8,128)S(1)} %bitcast.10, s32[8,128]{1,0:T(8,128)S(1)} %bitcast.12, s32[8,128]{1,0:T(8,128)S(1)} %bitcast.13, f32[3,8,128]{2,1,0:T(8,128)S(1)} %bitcast.11, f32[6,6,32]{2,1,0:T(8,128)S(1)} %copy-done), custom_call_target="tpu_custom_call" | custom-call | tf_op jit(solution)/shard_map/pallas_call | solution.py:364
  67.7 0.6 copy.11
  68.3 0.6 copy.12
Async XLA Ops:
  0.6 0.7 copy-start.5
  0.6 0.7 %copy-start.4 = (s32[1,8,128,1]{2,3,1,0:T(1,128)S(1)}, s32[1,8,128,1]{2,3,1,0:T(1,128)}, u32[]{:S(2)}) copy-start(s32[1,8,128,1]{2,3,1,0:T(1,128)} %param.8) | copy-start | bytes 12292
  1.3 0.7 %copy-start = (f32[6,6,32]{2,1,0:T(8,128)S(1)}, f32[6,6,32]{2,1,0:T(8,128)}, u32[]{:S(2)}) copy-start(f32[6,6,32]{2,1,0:T(8,128)} %inv_ref.1) | copy-start | bytes 13828
  2.1 0.7 %copy-start.1 = (f32[3,1,8,128]{3,2,1,0:T(8,128)S(1)}, f32[3,1,8,128]{3,2,1,0:T(8,128)}, u32[]{:S(2)}) copy-start(f32[3,1,8,128]{3,2,1,0:T(8,128)} %param.6) | copy-start | bytes 36868
  2.8 0.7 %copy-start.2 = (f32[3,1,8,128]{3,2,1,0:T(8,128)S(1)}, f32[3,1,8,128]{3,2,1,0:T(8,128)}, u32[]{:S(2)}) copy-start(f32[3,1,8,128]{3,2,1,0:T(8,128)} %param.7) | copy-start | bytes 36868
  3.5 0.7 %copy-start.3 = (f32[3,1,8,128]{3,2,1,0:T(8,128)S(1)}, f32[3,1,8,128]{3,2,1,0:T(8,128)}, u32[]{:S(2)}) copy-start(f32[3,1,8,128]{3,2,1,0:T(8,128)} %param.10) | copy-start | bytes 36868

commit v2 on v1

--- a/solution.py
+++ b/solution.py
@@ -215,7 +215,6 @@
 
     for copy in first_halo:
         copy.wait()
-    lax.fori_loop(0, tiles // 2, coefficients, 0)
     line, (beta2,) = received(1)
     beta = jnp.sqrt(beta2)
     motions = [solve_motion(line) / beta]
@@ -231,7 +230,7 @@
         return carry
 
     lax.fori_loop(0, ext // group, make_hot, 0)
-    lax.fori_loop(tiles // 2, tiles, coefficients, 0)
+    lax.fori_loop(0, tiles, coefficients, 0)
 
     def precondition(j):
         wait_motions()
@@ -258,12 +257,13 @@
                     movx[j, tile, c : c + 1, :] = vext[j, tile, c : c + 1, :] + extra[c]
             return carry
 
-        lax.fori_loop(0, ext // group, body, 0)
+        for chunk in range(ext // group):
+            body(chunk, 0)
 
     def mobility(j, slot):
         def body(t, carry):
             def part(q, carry):
-                here = pl.ds(pl.multiple_of(q * CHUNK, CHUNK), CHUNK)
+                here = slice(q * CHUNK, (q + 1) * CHUNK)
                 sums = [jnp.zeros((CHUNK, lanes), F32) for c in range(3)]
                 for code in range(9):
                     tile = (code // 3) * next_row + code % 3 + t
@@ -273,16 +273,18 @@
                     along = unit[0] * force[0] + unit[1] * force[1] + unit[2] * force[2]
                     sums = [sums[c] + (near * force[c] + along * unit[c]) for c in range(3)]
                 for c in range(3):
-                    acc[c, here, :] = sums[c]
+                    acc[3 * t + c, here, :] = sums[c]
                 return carry
 
-            lax.fori_loop(0, lanes // CHUNK, part, 0)
+            for q in range(lanes // CHUNK):
+                part(q, 0)
+            return carry
+
+        lax.fori_loop(0, tiles, body, 0)
+        for t in range(tiles):
             for c in range(3):
-                line = jnp.sum(acc[c].T, axis=0, keepdims=True)
+                line = jnp.sum(acc[3 * t + c].T, axis=0, keepdims=True)
                 wext[slot, base + t, c : c + 1, :] = movx[j, base + t, c : c + 1, :] + factor * line
-            return carry
-
-        lax.fori_loop(0, tiles, body, 0)
 
     hessen = []
     for j in range(ITERS):
@@ -376,7 +378,7 @@
             pltpu.VMEM((ITERS, ext, 4, lanes), F32),
             pltpu.VMEM((ext // group, 2 * ndev, group * lanes), BF16),
             pltpu.VMEM((tiles, 3, lanes, lanes), F32),
-            pltpu.VMEM((3, lanes, lanes), F32),
+            pltpu.VMEM((3 * tiles, lanes, lanes), F32),
             pltpu.VMEM((9 * tiles, 4, lanes, lanes), F32),
             pltpu.VMEM((width, width), F32),
             pltpu.VMEM((width, width), F32),

time: 69.4 us -> 64.4 us (0.928)
  Pallas kernels: 63.5 us -> 58.5 us
    pallas_call x1, Pallas kernels: 63.5 us -> 58.5 us  [local(): pl.pallas_call(functools.partial(kernel, ncell, nwide), out_shape=(jax.Sh...]
where the time goes in v2:
time: 64.4 us; the launch traced here: 63.9 us
  Pallas kernels  58.5 us (91%)
  local copies, waits for them, and re-layouts  4.74 us (7%)
  between operations  0.66 us (1%)
    pallas_call x1, Pallas kernels, local(): pl.pallas_call(functools.partial(kernel, ncell, nwide), out_shape=(jax.Sh...  58.5 us
    unnamed x14, local copies, waits for them, and re-layouts  4.74 us

profile of v2, /device:TPU:0, one launch (start us, length us, event | category | flops | bytes accessed | tf_op | source)
XLA Modules:
  0.0 63.9 jit_solution(13055187068163865592)
XLA Ops:
  0.6 0.0 copy-start.5
  0.6 0.0 copy-start.4
  0.7 0.7 %copy-done.5 = s32[1,8,128]{2,1,0:T(8,128)S(1)} copy-done((s32[1,8,128]{2,1,0:T(8,128)S(1)}, s32[1,8,128]{2,1,0:T(8,128)}, u32[]{:S(2)}) %copy-start.5) | copy-done | bytes 4120
  1.3 0.0 copy-done.4
  1.3 0.0 copy-start
  1.3 0.7 %copy-done = f32[6,6,32]{2,1,0:T(8,128)S(1)} copy-done((f32[6,6,32]{2,1,0:T(8,128)S(1)}, f32[6,6,32]{2,1,0:T(8,128)}, u32[]{:S(2)}) %copy-start) | copy-done | bytes 4632
  2.1 0.0 copy-start.1
  2.1 0.7 %copy-done.1 = f32[3,1,8,128]{3,2,1,0:T(8,128)S(1)} copy-done((f32[3,1,8,128]{3,2,1,0:T(8,128)S(1)}, f32[3,1,8,128]{3,2,1,0:T(8,128)}, u32[]{:S(2)}) %copy-start.1) | copy-done | bytes 12312
  2.8 0.0 copy-start.2
  2.8 0.7 %copy-done.2 = f32[3,1,8,128]{3,2,1,0:T(8,128)S(1)} copy-done((f32[3,1,8,128]{3,2,1,0:T(8,128)S(1)}, f32[3,1,8,128]{3,2,1,0:T(8,128)}, u32[]{:S(2)}) %copy-start.2) | copy-done | bytes 12312
  3.5 0.0 copy-start.3
  3.5 0.7 %copy-done.3 = f32[3,1,8,128]{3,2,1,0:T(8,128)S(1)} copy-done((f32[3,1,8,128]{3,2,1,0:T(8,128)S(1)}, f32[3,1,8,128]{3,2,1,0:T(8,128)}, u32[]{:S(2)}) %copy-start.3) | copy-done | bytes 12312
  4.2 58.5 %shard_map.77 = (f32[3,8,128]{2,1,0:T(8,128)S(1)}, f32[6,32]{1,0:T(8,128)S(1)}) custom-call(f32[3,8,128]{2,1,0:T(8,128)S(1)} %bitcast.9, f32[3,8,128]{2,1,0:T(8,128)S(1)} %bitcast.10, s32[8,128]{1,0:T(8,128)S(1)} %bitcast.12, s32[8,128]{1,0:T(8,128)S(1)} %bitcast.13, f32[3,8,128]{2,1,0:T(8,128)S(1)} %bitcast.11, f32[6,6,32]{2,1,0:T(8,128)S(1)} %copy-done), custom_call_target="tpu_custom_call" | custom-call | tf_op jit(solution)/shard_map/pallas_call | solution.py:366
  62.7 0.6 copy.11
  63.3 0.6 copy.12
Async XLA Ops:
  0.6 0.7 %copy-start.5 = (s32[1,8,128]{2,1,0:T(8,128)S(1)}, s32[1,8,128]{2,1,0:T(8,128)}, u32[]{:S(2)}) copy-start(s32[1,8,128]{2,1,0:T(8,128)} %param.9) | copy-start | bytes 12292
  0.6 0.7 %copy-start.4 = (s32[1,8,128,1]{2,3,1,0:T(1,128)S(1)}, s32[1,8,128,1]{2,3,1,0:T(1,128)}, u32[]{:S(2)}) copy-start(s32[1,8,128,1]{2,3,1,0:T(1,128)} %param.8) | copy-start | bytes 12292
  1.3 0.7 %copy-start = (f32[6,6,32]{2,1,0:T(8,128)S(1)}, f32[6,6,32]{2,1,0:T(8,128)}, u32[]{:S(2)}) copy-start(f32[6,6,32]{2,1,0:T(8,128)} %inv_ref.1) | copy-start | bytes 13828
  2.1 0.7 %copy-start.1 = (f32[3,1,8,128]{3,2,1,0:T(8,128)S(1)}, f32[3,1,8,128]{3,2,1,0:T(8,128)}, u32[]{:S(2)}) copy-start(f32[3,1,8,128]{3,2,1,0:T(8,128)} %param.6) | copy-start | bytes 36868
  2.8 0.7 %copy-start.2 = (f32[3,1,8,128]{3,2,1,0:T(8,128)S(1)}, f32[3,1,8,128]{3,2,1,0:T(8,128)}, u32[]{:S(2)}) copy-start(f32[3,1,8,128]{3,2,1,0:T(8,128)} %param.7) | copy-start | bytes 36868
  3.5 0.7 %copy-start.3 = (f32[3,1,8,128]{3,2,1,0:T(8,128)S(1)}, f32[3,1,8,128]{3,2,1,0:T(8,128)}, u32[]{:S(2)}) copy-start(f32[3,1,8,128]{3,2,1,0:T(8,128)} %param.10) | copy-start | bytes 36868
